TPU v7x, 128 devices: a whole 4x4x4 slice. The times are simulated.
128 devices in a mesh: ctx: 16 (over z, x), tp: 8 (over y, core).
Axes of the slice: x: 4, y: 4, z: 4, core: 2. Of those that a mesh axis runs over, the one named last changes fastest.
Arguments:
- hidden_in: bfloat16 [8192, 5376], P(('ctx', 'tp')), may hold values from -6 to 6
- stretch_start: int32 [1], replicated, may hold values from 1 to 1024
- pre_gain: float32 [5376], replicated, may hold values from 0.1 to 1.9
- q_weight: bfloat16 [5376, 4096], P('ctx', 'tp'), may hold values from -1 to 1
- k_weight: bfloat16 [5376, 2048], P('ctx', 'tp'), may hold values from -1 to 1
- v_weight: bfloat16 [5376, 2048], P('ctx', 'tp'), may hold values from -0.078125 to 0.078125
- o_weight: bfloat16 [4096, 5376], P('tp', 'ctx'), may hold values from -0.09375 to 0.09375
- q_gain: float32 [128], replicated, may hold values from 0.5 to 5
- k_gain: float32 [128], replicated, may hold values from 0.5 to 5
- prior_keys: bfloat16 [1024, 2048], P(None, 'tp'), may hold values from -6 to 6
- prior_values: bfloat16 [1024, 2048], P(None, 'tp'), may hold values from -6 to 6
- post_gain: float32 [5376], replicated, may hold values from 0.1 to 1.9
Outputs:
- result: bfloat16 [8192, 5376], P(('ctx', 'tp'))
All inputs are finite; a program needn't handle non-finite values.
Results may differ from a plain program's by a relative error of at most 0.013.
Values may be sent and summed in bfloat16 or wider, within the bound.
A program may use at most 128 MiB of HBM per device.

v0:
```python
import jax
import jax.numpy as jnp
from jax import lax
from jax.sharding import PartitionSpec as P

HD = 128
WINDOW = 1024
EPSILON = 1e-06
QUERY_FACTOR = 168.0 ** (-0.5)


def in_one_piece(arrays, axis, dim, along):
    ends, at = ([], 0)
    for a in arrays[:-1]:
        at += a.shape[along]
        ends.append(at)
    both = jnp.concatenate(arrays, axis=along)
    return tuple(jnp.split(lax.all_gather(both, axis, axis=dim, tiled=True), ends, axis=along))


def from_behind(value, axis, steps):
    count = lax.axis_size(axis)
    leading, last = (max(0, -steps), min(count, count - steps))
    return lax.ppermute(value, axis, [(source, source + steps) for source in range(leading, last)])


def rms_scale(inputs, scales):
    mean_sq = jnp.mean(inputs * inputs, axis=-1, keepdims=True)
    return inputs * lax.rsqrt(mean_sq + EPSILON) * scales


def rotate(inputs, positions):
    half_dim = inputs.shape[-1] // 2
    frequency = 10000.0 ** (-jnp.arange(half_dim, dtype=jnp.float32) / half_dim)
    angles = positions.astype(jnp.float32)[:, None] * frequency[None, :]
    cosines = jnp.cos(angles)[:, None, :]
    sines = jnp.sin(angles)[:, None, :]
    front = inputs[..., :half_dim]
    second = inputs[..., half_dim:]
    return jnp.concatenate(
        [front * cosines - second * sines, second * cosines + front * sines], axis=-1
    )


def local(
    hidden_in,
    stretch_start,
    pre_gain,
    q_weight,
    k_weight,
    v_weight,
    o_weight,
    q_gain,
    k_gain,
    prior_keys,
    prior_values,
    post_gain,
):
    residual_in = hidden_in.astype(jnp.float32)
    normed = rms_scale(residual_in, pre_gain).astype(jnp.bfloat16)
    block_rows = lax.all_gather(normed, "tp", axis=0, tiled=True)
    row_count = block_rows.shape[0]
    query_cols = q_weight.shape[1]
    kv_cols = k_weight.shape[1]

    def add_piece(segment):
        return jnp.dot(block_rows, segment, preferred_element_type=jnp.float32)

    segments = in_one_piece((q_weight, k_weight, v_weight), "ctx", 0, 1)
    query_raw, key_raw, value_raw = tuple((add_piece(segment) for segment in segments))
    local_heads = query_cols // HD
    local_kv = kv_cols // HD
    group = local_heads // local_kv
    chain_pos = lax.axis_index("ctx")
    positions = WINDOW + chain_pos * row_count + jnp.arange(row_count, dtype=jnp.int32)
    query = (
        rotate(rms_scale(query_raw.reshape(row_count, local_heads, HD), q_gain), positions)
        * QUERY_FACTOR
    ).astype(jnp.bfloat16)
    key_rows = (
        rotate(rms_scale(key_raw.reshape(row_count, local_kv, HD), k_gain), positions)
        .astype(jnp.bfloat16)
        .reshape(row_count, kv_cols)
    )
    value_rows = value_raw.astype(jnp.bfloat16)
    reach = WINDOW // row_count
    earlier = []
    current = (key_rows, value_rows)
    for hop_index in range(reach):
        current = from_behind((current[0], current[1]), "ctx", 1)
        earlier.append(current)
    key_parts = []
    value_parts = []
    for hop_index in range(reach - 1, -1, -1):
        source = chain_pos - (hop_index + 1)
        offset = jnp.maximum(WINDOW + source * row_count, 0)
        cached_keys = lax.dynamic_slice_in_dim(prior_keys, offset, row_count, 0)
        cached_values = lax.dynamic_slice_in_dim(prior_values, offset, row_count, 0)
        key_parts.append(jnp.where(source < 0, cached_keys, earlier[hop_index][0]))
        value_parts.append(jnp.where(source < 0, cached_values, earlier[hop_index][1]))
    key_parts.append(key_rows)
    value_parts.append(value_rows)
    span = (reach + 1) * row_count
    all_keys = jnp.concatenate(key_parts, axis=0).reshape(span, local_kv, HD)
    all_values = jnp.concatenate(value_parts, axis=0).reshape(span, local_kv, HD)
    key_anchor = WINDOW + (chain_pos - reach) * row_count
    query_grouped = query.reshape(row_count, local_kv, group, HD)
    scores = jnp.einsum(
        "qhgd,khd->hgqk", query_grouped, all_keys, preferred_element_type=jnp.float32
    )
    key_pos = key_anchor + jnp.arange(span, dtype=jnp.int32)
    first_valid = WINDOW - stretch_start[0]
    allowed = (
        (key_pos[None, :] <= positions[:, None])
        & (key_pos[None, :] > positions[:, None] - WINDOW)
        & (key_pos[None, :] >= first_valid)
    )
    scores = jnp.where(allowed[None, None, :, :], scores, jnp.float32(-1e30))
    largest = jnp.max(scores, axis=-1, keepdims=True)
    expon = jnp.exp(scores - largest)
    attn_probs = (expon / jnp.sum(expon, axis=-1, keepdims=True)).astype(jnp.bfloat16)
    attended = jnp.einsum(
        "hgqk,khd->qhgd", attn_probs, all_values, preferred_element_type=jnp.float32
    )
    attended = attended.astype(jnp.bfloat16).reshape(row_count, query_cols)
    partial_rows = jnp.dot(
        attended,
        lax.all_gather(o_weight, "ctx", axis=1, tiled=True),
        preferred_element_type=jnp.float32,
    )
    summed = lax.psum_scatter(
        partial_rows.astype(jnp.bfloat16), "tp", scatter_dimension=0, tiled=True
    ).astype(jnp.float32)
    return (residual_in + rms_scale(summed, post_gain)).astype(jnp.bfloat16)


def solution(mesh):
    return jax.shard_map(
        local,
        mesh=mesh,
        in_specs=(
            P(("ctx", "tp"), None),
            P(),
            P(),
            P("ctx", "tp"),
            P("ctx", "tp"),
            P("ctx", "tp"),
            P("tp", "ctx"),
            P(),
            P(),
            P(None, "tp"),
            P(None, "tp"),
            P(),
        ),
        out_specs=P(("ctx", "tp"), None),
        check_vma=False,
    )
```

profile of v0, /device:TPU:0, one launch (start us, length us, event | category | flops | bytes accessed | tf_op | source)
XLA Modules:
  0.0 256.0 jit_solution(17121036638809811373)
XLA Ops:
  6.5 1.3 fusion.15
  7.9 2.2 fusion.17
  10.1 2.1 pad_maximum_fusion.1
  14.6 1.9 and_and_fusion
  16.5 33.8 %all-gather.4.cloned.1.call-done = bf16[512,5376]{1,0:T(8,128)(2,1)} async-done(((bf16[64,5376]{1,0:T(8,128)(2,1)}), bf16[512,5376]{1,0:T(8,128)(2,1)}) %all-gather.4.cloned.1.call-update) | async-done | bytes 5505040 | tf_op jit(solution)/shard_map/all_gather | solution.py:61
  50.3 85.0 %all-gather.6.cloned.1.call-done = bf16[5376,1024]{1,0:T(8,128)(2,1)} async-done(((bf16[336,1024]{1,0:T(8,128)(2,1)}), bf16[5376,1024]{1,0:T(8,128)(2,1)}) %all-gather.6.cloned.1.call-update) | async-done | bytes 11010064 | tf_op jit(solution)/shard_map/all_gather | solution.py:18
  135.3 5.1 %fusion.20 = bf16[512,256]{1,0:T(8,128)(2,1)S(1)} fusion(bf16[512,5376]{1,0:T(8,128)(2,1)} %all-gather.4.cloned.1.call-done, bf16[5376,1024]{1,0:T(8,128)(2,1)} %all-gather.6.cloned.1.call-done), kind=kOutput, calls=%fused_computation.29 | convolution fusion | flops 1409417216 | bytes 8519680 | tf_op jit(solution)/shard_map/dot_general | solution.py:67
  140.4 4.2 %collective-permute-start = (bf16[512,256]{1,0:T(8,128)(2,1)S(1)}, bf16[512,256]{1,0:T(8,128)(2,1)}, u32[]{:S(2)}, u32[]{:S(2)}) collective-permute-start(bf16[512,256]{1,0:T(8,128)(2,1)S(1)} %fusion.20), channel_id=1, source_target_pairs={{0,8},{8,16},{16,24},{24,32},{32,40},{40,48},{48,56},{56,64},{64,7... | collective-permute-start | bytes 786440 | tf_op jit(solution)/shard_map/ppermute | solution.py:24
  144.6 3.5 %multiply_reduce_fusion.1 = (f32[512,2]{0,1:T(2,128)S(1)}, f32[512,256]{0,1:T(8,128)S(1)}) fusion(bf16[512,5376]{1,0:T(8,128)(2,1)S(1)} %copy-done.7, bf16[5376,1024]{1,0:T(8,128)(2,1)} %all-gather.6.cloned.1.call-done), kind=kOutput, calls=%fused_computation.43 | convolution fusion | flops 1409547264 | bytes 8785920 | tf_op jit(solution)/shard_map/dot_general | solution.py:67
  149.7 3.5 %collective-permute-start.2 = (bf16[512,256]{1,0:T(8,128)(2,1)}, bf16[512,256]{1,0:T(8,128)(2,1)}, u32[]{:S(2)}, u32[]{:S(2)}) collective-permute-start(bf16[512,256]{1,0:T(8,128)(2,1)} %copy_bitcast_fusion), channel_id=1, source_target_pairs={{0,8},{8,16},{16,24},{24,32},{32,40},{40,48},{48,56},{56,64},{64,7... | collective-permute-start | bytes 786440 | tf_op jit(solution)/shard_map/ppermute | solution.py:24
  153.2 6.8 %multiply_reduce_fusion = (f32[512,4]{0,1:T(4,128)S(1)}, f32[512,512]{0,1:T(8,128)S(1)}) fusion(bf16[512,5376]{1,0:T(8,128)(2,1)} %all-gather.4.cloned.1.call-done, bf16[5376,1024]{1,0:T(8,128)(2,1)} %all-gather.6.cloned.1.call-done), kind=kOutput, calls=%fused_computation.33 | convolution fusion | flops 2819094528 | bytes 12066816 | tf_op jit(solution)/shard_map/dot_general | solution.py:67
  160.2 3.1 %collective-permute-start.1 = (bf16[512,256]{1,0:T(8,128)(2,1)}, bf16[512,256]{1,0:T(8,128)(2,1)}, u32[]{:S(2)}, u32[]{:S(2)}) collective-permute-start(bf16[512,256]{1,0:T(8,128)(2,1)} %collective-permute-done), channel_id=1, source_target_pairs={{0,8},{8,16},{16,24},{24,32},{32,40},{40,48},{48,56},{56,64},{64,7... | collective-permute-start | bytes 786440 | tf_op jit(solution)/shard_map/ppermute | solution.py:24
  165.1 3.2 %collective-permute-start.3 = (bf16[512,256]{1,0:T(8,128)(2,1)}, bf16[512,256]{1,0:T(8,128)(2,1)}, u32[]{:S(2)}, u32[]{:S(2)}) collective-permute-start(bf16[512,256]{1,0:T(8,128)(2,1)} %collective-permute-done.2), channel_id=1, source_target_pairs={{0,8},{8,16},{16,24},{24,32},{32,40},{40,48},{48,56},{56,64},{64,7... | collective-permute-start | bytes 786440 | tf_op jit(solution)/shard_map/ppermute | solution.py:24
  168.7 1.2 dynamic-slice_select_fusion.1
  170.0 1.1 pad_maximum_fusion
  171.0 1.2 copy.36
  172.2 5.2 %collective-permute-done.3 = bf16[512,256]{1,0:T(8,128)(2,1)} collective-permute-done((bf16[512,256]{1,0:T(8,128)(2,1)}, bf16[512,256]{1,0:T(8,128)(2,1)}, u32[]{:S(2)}, u32[]{:S(2)}) %collective-permute-start.3) | collective-permute-done | bytes 262176 | tf_op jit(solution)/shard_map/ppermute | solution.py:24
  177.7 10.2 %fusion.32 = (f32[2,2,512]{2,1,0:T(2,128)S(1)}, f32[2,2,512,1536]{2,3,1,0:T(8,128)}) fusion(pred[512,1536]{0,1:T(8,128)(4,1)} %and_and_fusion, bf16[512,2,128]{2,0,1:T(8,128)(2,1)} %maximum_convert_fusion, bf16[512,2,128]{2,0,1:T(8,128)(2,1)S(1)} %get-tuple-element.23, bf16[512,2,128]{2,0,1:T(8,128)(2,1)S(1)} %get-tuple-element.24, ...), kind=kOutput, calls=%fused_computation.67 | convolution fusion | flops 817890816 | bytes 15212544 | tf_op jit(solution)/shard_map/sub | solution.py:120
  187.9 5.8 %fusion.19 = bf16[2,128,2,512]{3,1,2,0:T(8,128)(2,1)S(1)} fusion(bf16[1536,2,128,1]{0,2,3,1:T(8,128)(2,1)S(1)} %bitcast.62, f32[2,2,512,1536]{2,3,1,0:T(8,128)} %get-tuple-element.20, f32[2,2,512]{2,1,0:T(2,128)S(1)} %get-tuple-element.19), kind=kOutput, calls=%fused_computation.28 | convolution fusion | flops 811859968 | bytes 13901824 | tf_op jit(solution)/shard_map/hgqk,khd->qhgd/dot_general | solution.py:122
  193.7 4.2 %all-gather.8.cloned.1.call-done = bf16[512,5376]{0,1:T(8,128)(2,1)} async-done(((bf16[512,336]{0,1:T(8,128)(2,1)}), bf16[512,5376]{0,1:T(8,128)(2,1)}) %all-gather.8.cloned.1.call-update) | async-done | bytes 5505040 | tf_op jit(solution)/shard_map/all_gather | solution.py:128
  197.9 7.5 %convolution_convert_fusion = bf16[512,5376]{1,0:T(8,128)(2,1)} fusion(bf16[512,512]{0,1:T(8,128)(2,1)S(1)} %bitcast.64, bf16[512,5376]{0,1:T(8,128)(2,1)} %all-gather.8.cloned.1.call-done), kind=kOutput, calls=%fused_computation.5 | convolution fusion | flops 2821324800 | bytes 11534336 | tf_op jit(solution)/shard_map/dot_general | solution.py:126
  205.5 40.4 %reduce-scatter.2.cloned.1.call-done = bf16[64,5376]{1,0:T(8,128)(2,1)} async-done(((bf16[512,5376]{1,0:T(8,128)(2,1)}), bf16[64,5376]{1,0:T(8,128)(2,1)}) %reduce-scatter.2.cloned.1.call-update) | async-done | bytes 688144 | tf_op jit(solution)/shard_map/reduce_scatter | solution.py:131
  245.8 1.3 fusion.13
  247.2 2.3 fusion.18
  (50 shorter events, 5.9 us)
Async XLA Ops:
  6.5 43.8 %all-gather.4.cloned.1.call-start = ((), (), s32[]{:S(2)}) async-start(), calls=%async_computation.1 | async-start | bytes 6193152 | tf_op jit(solution)/shard_map/all_gather | solution.py:61
  10.1 125.2 %all-gather.6.cloned.1.call-start = ((), (), s32[]{:S(2)}) async-start(), calls=%async_computation.2 | async-start | bytes 11698176 | tf_op jit(solution)/shard_map/all_gather | solution.py:18
  12.3 185.7 %all-gather.8.cloned.1.call-start = ((), (), s32[]{:S(2)}) async-start(), calls=%async_computation.3 | async-start | bytes 5849088 | tf_op jit(solution)/shard_map/all_gather | solution.py:128
  13.0 232.8 %reduce-scatter.2.cloned.1.call-start = ((), (), s32[]{:S(2)}) async-start(), calls=%async_computation.4 | async-start | bytes 6193152 | tf_op jit(solution)/shard_map/reduce_scatter | solution.py:131
  135.3 9.4 %copy-start.7 = (bf16[512,5376]{1,0:T(8,128)(2,1)S(1)}, bf16[512,5376]{1,0:T(8,128)(2,1)}, u32[]{:S(2)}) copy-start(bf16[512,5376]{1,0:T(8,128)(2,1)} %all-gather.4.cloned.1.call-done) | copy-start | bytes 16515076
  140.4 7.9 %copy-start.3 = (bf16[512,256]{1,0:T(8,128)(2,1)}, bf16[512,256]{1,0:T(8,128)(2,1)S(1)}, u32[]{:S(2)}) copy-start(bf16[512,256]{1,0:T(8,128)(2,1)S(1)} %fusion.20) | copy-start | bytes 786436
  140.4 7.9 %copy-start.5 = (f32[128]{0:T(128)S(1)}, f32[128]{0:T(128)}, u32[]{:S(2)}) copy-start(f32[128]{0:T(128)} %param.20) | copy-start | bytes 1540
  140.4 19.8 %collective-permute-start = (bf16[512,256]{1,0:T(8,128)(2,1)S(1)}, bf16[512,256]{1,0:T(8,128)(2,1)}, u32[]{:S(2)}, u32[]{:S(2)}) collective-permute-start(bf16[512,256]{1,0:T(8,128)(2,1)S(1)} %fusion.20), channel_id=1, source_target_pairs={{0,8},{8,16},{16,24},{24,32},{32,40},{40,48},{48,56},{56,64},{64,7... | collective-permute-start | bytes 786440 | tf_op jit(solution)/shard_map/ppermute | solution.py:24
  149.7 10.3 %copy-start.6 = (f32[128]{0:T(128)S(1)}, f32[128]{0:T(128)}, u32[]{:S(2)}) copy-start(f32[128]{0:T(128)} %param.19) | copy-start | bytes 1540
  149.7 15.4 %collective-permute-start.2 = (bf16[512,256]{1,0:T(8,128)(2,1)}, bf16[512,256]{1,0:T(8,128)(2,1)}, u32[]{:S(2)}, u32[]{:S(2)}) collective-permute-start(bf16[512,256]{1,0:T(8,128)(2,1)} %copy_bitcast_fusion), channel_id=1, source_target_pairs={{0,8},{8,16},{16,24},{24,32},{32,40},{40,48},{48,56},{56,64},{64,7... | collective-permute-start | bytes 786440 | tf_op jit(solution)/shard_map/ppermute | solution.py:24
  160.2 8.5 %collective-permute-start.1 = (bf16[512,256]{1,0:T(8,128)(2,1)}, bf16[512,256]{1,0:T(8,128)(2,1)}, u32[]{:S(2)}, u32[]{:S(2)}) collective-permute-start(bf16[512,256]{1,0:T(8,128)(2,1)} %collective-permute-done), channel_id=1, source_target_pairs={{0,8},{8,16},{16,24},{24,32},{32,40},{40,48},{48,56},{56,64},{64,7... | collective-permute-start | bytes 786440 | tf_op jit(solution)/shard_map/ppermute | solution.py:24
  164.2 13.2 %copy-start.2 = (bf16[1024,256]{1,0:T(8,128)(2,1)S(1)}, bf16[1024,256]{1,0:T(8,128)(2,1)}, u32[]{:S(2)}) copy-start(bf16[1024,256]{1,0:T(8,128)(2,1)} %param.21) | copy-start | bytes 1572868
  165.1 12.3 %collective-permute-start.3 = (bf16[512,256]{1,0:T(8,128)(2,1)}, bf16[512,256]{1,0:T(8,128)(2,1)}, u32[]{:S(2)}, u32[]{:S(2)}) collective-permute-start(bf16[512,256]{1,0:T(8,128)(2,1)} %collective-permute-done.2), channel_id=1, source_target_pairs={{0,8},{8,16},{16,24},{24,32},{32,40},{40,48},{48,56},{56,64},{64,7... | collective-permute-start | bytes 786440 | tf_op jit(solution)/shard_map/ppermute | solution.py:24
  177.7 10.2 %copy-start.1 = (bf16[1536,256]{0,1:T(8,128)(2,1)S(1)}, bf16[1536,256]{0,1:T(8,128)(2,1)}, u32[]{:S(2)}) copy-start(bf16[1536,256]{0,1:T(8,128)(2,1)} %copy.36) | copy-start | bytes 2359300
  205.5 41.7 %copy-start = (bf16[64,5376]{1,0:T(8,128)(2,1)S(1)}, bf16[64,5376]{1,0:T(8,128)(2,1)}, u32[]{:S(2)}) copy-start(bf16[64,5376]{1,0:T(8,128)(2,1)} %param.12) | copy-start | bytes 2064388
  205.5 41.7 %copy-start.4 = (f32[5376]{0:T(1024)S(1)}, f32[5376]{0:T(1024)}, u32[]{:S(2)}) copy-start(f32[5376]{0:T(1024)} %param.23) | copy-start | bytes 64516
Sparse Core Ops, SparseCore 0:
  10.2 40.0 all-gather.3
  52.4 82.7 all-gather.5
  137.4 60.4 all-gather.7
  205.6 40.1 reduce-scatter.1
where the time goes:
time: 257 us; the launch traced here: 256 us
  waiting for transfers between devices  170 us (66%)
  matrix products  38.9 us (15%)
  other arithmetic  16.7 us (6%)
  starting transfers between devices  14.1 us (5%)
  between operations  14 us (5%)
    all_gather x1, waiting for transfers between devices, in_one_piece(): lax.all_gather(both, axis, axis=dim, tiled=True)  85 us
    reduce_scatter x1, waiting for transfers between devices, local(): lax.psum_scatter(partial_rows.astype(jnp.bfloat16), 'tp', scatter_dimensi...  40.4 us
    all_gather x1, waiting for transfers between devices, local(): block_rows = lax.all_gather(normed, 'tp', axis=0, tiled=True)  33.8 us
    dot_general x3, matrix products, add_piece(): return jnp.dot(block_rows, segment, preferred_element_type=jnp.float32)  15.4 us
    ppermute x4, starting transfers between devices, from_behind(): lax.ppermute(value, axis, [(source, source + steps) for source in range(l...  14 us
    sub x1, matrix products, local(): expon = jnp.exp(scores - largest)  10.2 us
    dot_general x1, matrix products, local(): jnp.dot(attended, lax.all_gather(o_weight, 'ctx', axis=1, tiled=True), pr...  7.51 us
    dot_general x1, matrix products, local(): jnp.einsum('hgqk,khd->qhgd', attn_probs, all_values, preferred_element_ty...  5.77 us
  transfers between devices with their start and end apart: 8, of which 6 were waited for; matrix products, arithmetic and copies ran while one was open for 17% of the time, Pallas kernels for 0%

commit v1 on v0

--- a/solution.py
+++ b/solution.py
@@ -58,7 +58,9 @@
 ):
     residual_in = hidden_in.astype(jnp.float32)
     normed = rms_scale(residual_in, pre_gain).astype(jnp.bfloat16)
-    block_rows = lax.all_gather(normed, "tp", axis=0, tiled=True)
+    block_rows = jnp.concatenate(
+        lax.all_to_all(jnp.stack([normed] * lax.axis_size("tp")), "tp", 0, 0), axis=0
+    )
     row_count = block_rows.shape[0]
     query_cols = q_weight.shape[1]
     kv_cols = k_weight.shape[1]

time: 257 us -> 248 us (0.965)
  waiting for transfers between devices: 170 us -> 134 us
  local copies, waits for them, and re-layouts: 2.41 us -> 24.8 us
  starting transfers between devices: 14.1 us -> 18.5 us
    all_gather x1 -> x0, waiting for transfers between devices: 33.8 us -> none  [local(): block_rows = lax.all_gather(normed, 'tp', axis=0, tiled=True)]
    dot_general x0 -> x4, local copies, waits for them, and re-layouts: none -> 18.3 us  [add_piece(): return jnp.dot(block_rows, segment, preferred_element_type=jnp.float32)]
    all_gather x1, waiting for transfers between devices: 85 us -> 72 us  [in_one_piece(): lax.all_gather(both, axis, axis=dim, tiled=True)]
    ppermute x4, waiting for transfers between devices: 5.67 us -> 18.5 us  [from_behind(): lax.ppermute(value, axis, [(source, source + steps) for source in range(l...]
    all_to_all x0 -> x1, starting transfers between devices: none -> 4.67 us  [local(): lax.all_to_all(jnp.stack([normed] * lax.axis_size('tp')), 'tp', 0, 0)]
    all_gather x1, waiting for transfers between devices: 4.23 us -> 0.02 us  [local(): lax.all_gather(o_weight, 'ctx', axis=1, tiled=True)]
    another operation x0 -> x1, local copies, waits for them, and re-layouts: none -> 2.83 us  [local(): jnp.stack([normed] * lax.axis_size('tp'))]
  transfers between devices with their start and end apart: 8 -> 8, of which waited for: 6 -> 4; matrix products, arithmetic and copies ran while one was open for 17% -> 27% of each run, Pallas kernels for 0% -> 0%
where the time goes in v1:
time: 248 us; the launch traced here: 247 us
  waiting for transfers between devices  134 us (54%)
  matrix products  40.5 us (16%)
  local copies, waits for them, and re-layouts  24.8 us (10%)
  starting transfers between devices  18.5 us (7%)
  other arithmetic  14.8 us (6%)
  between operations  14 us (6%)
    all_gather x1, waiting for transfers between devices, in_one_piece(): lax.all_gather(both, axis, axis=dim, tiled=True)  72 us
    reduce_scatter x1, waiting for transfers between devices, local(): lax.psum_scatter(partial_rows.astype(jnp.bfloat16), 'tp', scatter_dimensi...  42.8 us
    ppermute x4, waiting for transfers between devices, from_behind(): lax.ppermute(value, axis, [(source, source + steps) for source in range(l...  18.5 us
    dot_general x4, local copies, waits for them, and re-layouts, add_piece(): return jnp.dot(block_rows, segment, preferred_element_type=jnp.float32)  18.3 us
    dot_general x3, matrix products, add_piece(): return jnp.dot(block_rows, segment, preferred_element_type=jnp.float32)  16.7 us
    ppermute x4, starting transfers between devices, from_behind(): lax.ppermute(value, axis, [(source, source + steps) for source in range(l...  13.8 us
    sub x1, matrix products, local(): expon = jnp.exp(scores - largest)  10.7 us
    dot_general x1, matrix products, local(): jnp.dot(attended, lax.all_gather(o_weight, 'ctx', axis=1, tiled=True), pr...  7.55 us
  transfers between devices with their start and end apart: 8, of which 4 were waited for; matrix products, arithmetic and copies ran while one was open for 27% of the time, Pallas kernels for 0%

profile of v1, /device:TPU:0, one launch (start us, length us, event | category | flops | bytes accessed | tf_op | source)
XLA Modules:
  0.0 246.7 jit_solution(16467699194326733964)
XLA Ops:
  6.5 2.1 pad_maximum_fusion.1
  11.3 2.8 %stack.2 = bf16[8,64,5376]{2,1,0:T(8,128)(2,1)} broadcast(bf16[64,5376]{1,0:T(8,128)(2,1)S(1)} %fusion.13), dimensions={1,2} | broadcast | bytes 6193152 | tf_op jit(solution)/shard_map/stack | solution.py:62
  14.2 4.7 %all-to-all-start = ((bf16[8,64,5376]{2,1,0:T(8,128)(2,1)}), bf16[8,64,5376]{2,1,0:T(8,128)(2,1)}, u32[]{:S(2)}, u32[]{:S(2)}) async-start(bf16[8,64,5376]{2,1,0:T(8,128)(2,1)} %stack.2), calls=%async_computation | async-start | bytes 11010048 | tf_op jit(solution)/shard_map/all_to_all | solution.py:62
  20.9 1.9 and_and_fusion
  22.8 72.0 %all-gather.3.cloned.1.call-done = bf16[5376,1024]{1,0:T(8,128)(2,1)} async-done(((bf16[336,1024]{1,0:T(8,128)(2,1)}), bf16[5376,1024]{1,0:T(8,128)(2,1)}) %all-gather.3.cloned.1.call-update) | async-done | bytes 11010064 | tf_op jit(solution)/shard_map/all_gather | solution.py:18
  94.8 2.0 slice_bitcast_fusion.1
  96.7 3.0 %copy.13 = bf16[256,5376]{1,0:T(8,128)(2,1)} copy(bf16[256,5376]{0,1:T(8,128)(2,1)S(1)} %slice_bitcast_fusion.1) | data formatting | bytes 5505024 | tf_op jit(solution)/shard_map/dot_general | solution.py:69
  99.7 5.0 %multiply_reduce_fusion.1 = (f32[512,2]{0,1:T(2,128)S(1)}, f32[512,2,128]{0,2,1:T(8,128)S(1)}) fusion(bf16[512,5376,1]{1,0,2:T(8,128)(2,1)} %bitcast.5, bf16[2,128,5376]{2,1,0:T(8,128)(2,1)} %bitcast.57), kind=kOutput, calls=%fused_computation.39 | convolution fusion | flops 1409547264 | bytes 8785920 | tf_op jit(solution)/shard_map/dot_general | solution.py:69
  105.2 4.1 %collective-permute-start.2 = (bf16[512,256]{1,0:T(8,128)(2,1)S(1)}, bf16[512,256]{1,0:T(8,128)(2,1)}, u32[]{:S(2)}, u32[]{:S(2)}) collective-permute-start(bf16[512,256]{1,0:T(8,128)(2,1)S(1)} %copy.27), channel_id=1, source_target_pairs={{0,8},{8,16},{16,24},{24,32},{32,40},{40,48},{48,56},{56,64},{64,7... | collective-permute-start | bytes 786440 | tf_op jit(solution)/shard_map/ppermute | solution.py:24
  109.3 5.0 %fusion.16 = bf16[512,256]{1,0:T(8,128)(2,1)S(1)} fusion(bf16[512,5376]{1,0:T(8,128)(2,1)} %bitcast, bf16[5376,1024]{1,0:T(8,128)(2,1)} %all-gather.3.cloned.1.call-done), kind=kOutput, calls=%fused_computation.27 | convolution fusion | flops 1409417216 | bytes 8519680 | tf_op jit(solution)/shard_map/dot_general | solution.py:69
  114.3 3.4 %collective-permute-start = (bf16[512,256]{1,0:T(8,128)(2,1)S(1)}, bf16[512,256]{1,0:T(8,128)(2,1)}, u32[]{:S(2)}, u32[]{:S(2)}) collective-permute-start(bf16[512,256]{1,0:T(8,128)(2,1)S(1)} %fusion.16), channel_id=1, source_target_pairs={{0,8},{8,16},{16,24},{24,32},{32,40},{40,48},{48,56},{56,64},{64,7... | collective-permute-start | bytes 786440 | tf_op jit(solution)/shard_map/ppermute | solution.py:24
  117.7 5.4 %slice_bitcast_fusion = bf16[512,5376]{0,1:T(8,128)(2,1)} fusion(bf16[5376,1024]{1,0:T(8,128)(2,1)} %all-gather.3.cloned.1.call-done), kind=kLoop, calls=%fused_computation.10 | loop fusion | bytes 11010048 | tf_op jit(solution)/shard_map/dot_general | solution.py:69
  123.0 8.0 %copy.17 = bf16[512,5376]{1,0:T(8,128)(2,1)} copy(bf16[512,5376]{0,1:T(8,128)(2,1)} %slice_bitcast_fusion) | data formatting | bytes 11010048 | tf_op jit(solution)/shard_map/dot_general | solution.py:69
  131.1 6.7 %multiply_reduce_fusion = (f32[512,4]{0,1:T(4,128)S(1)}, f32[512,4,128]{0,2,1:T(8,128)S(1)}) fusion(bf16[512,5376,1]{1,0,2:T(8,128)(2,1)} %bitcast.5, bf16[4,128,5376]{2,1,0:T(8,128)(2,1)} %bitcast.56), kind=kOutput, calls=%fused_computation.31 | convolution fusion | flops 2819094528 | bytes 12066816 | tf_op jit(solution)/shard_map/dot_general | solution.py:69
  138.0 3.1 %collective-permute-start.3 = (bf16[512,256]{1,0:T(8,128)(2,1)}, bf16[512,256]{1,0:T(8,128)(2,1)}, u32[]{:S(2)}, u32[]{:S(2)}) collective-permute-start(bf16[512,256]{1,0:T(8,128)(2,1)} %collective-permute-done.2), channel_id=1, source_target_pairs={{0,8},{8,16},{16,24},{24,32},{32,40},{40,48},{48,56},{56,64},{64,7... | collective-permute-start | bytes 786440 | tf_op jit(solution)/shard_map/ppermute | solution.py:24
  141.1 3.2 %collective-permute-start.1 = (bf16[512,256]{1,0:T(8,128)(2,1)}, bf16[512,256]{1,0:T(8,128)(2,1)}, u32[]{:S(2)}, u32[]{:S(2)}) collective-permute-start(bf16[512,256]{1,0:T(8,128)(2,1)} %collective-permute-done), channel_id=1, source_target_pairs={{0,8},{8,16},{16,24},{24,32},{32,40},{40,48},{48,56},{56,64},{64,7... | collective-permute-start | bytes 786440 | tf_op jit(solution)/shard_map/ppermute | solution.py:24
  145.2 7.8 %collective-permute-done.3 = bf16[512,256]{1,0:T(8,128)(2,1)} collective-permute-done((bf16[512,256]{1,0:T(8,128)(2,1)}, bf16[512,256]{1,0:T(8,128)(2,1)}, u32[]{:S(2)}, u32[]{:S(2)}) %collective-permute-start.3) | collective-permute-done | bytes 262176 | tf_op jit(solution)/shard_map/ppermute | solution.py:24
  153.0 10.7 %collective-permute-done.1 = bf16[512,256]{1,0:T(8,128)(2,1)} collective-permute-done((bf16[512,256]{1,0:T(8,128)(2,1)}, bf16[512,256]{1,0:T(8,128)(2,1)}, u32[]{:S(2)}, u32[]{:S(2)}) %collective-permute-start.1) | collective-permute-done | bytes 262176 | tf_op jit(solution)/shard_map/ppermute | solution.py:24
  163.7 2.3 dynamic-slice_select_fusion.1
  169.9 10.7 %fusion.28 = (f32[2,2,512]{2,1,0:T(2,128)S(1)}, f32[2,2,512,1536]{2,3,1,0:T(8,128)}) fusion(pred[512,1536]{0,1:T(8,128)(4,1)} %and_and_fusion, bf16[512,2,128]{0,2,1:T(8,128)(2,1)S(1)} %maximum_convert_fusion, bf16[512,2,128]{0,2,1:T(8,128)(2,1)} %bitcast.62, bf16[512,2,128]{0,2,1:T(8,128)(2,1)} %bitcast.63, f32[512,2,2,64]{3,0,2,1:T(8,128)S(1)} %copy.19, ...), kind=kOutput, calls=%fused_computation.62 | convolution fusion | flops 817890816 | bytes 15212544 | tf_op jit(solution)/shard_map/sub | solution.py:122
  180.6 5.6 %fusion.15 = bf16[2,128,2,512]{3,1,2,0:T(8,128)(2,1)S(1)} fusion(bf16[1536,2,128,1]{0,2,3,1:T(8,128)(2,1)S(1)} %bitcast.61, f32[2,2,512,1536]{2,3,1,0:T(8,128)} %get-tuple-element.20, f32[2,2,512]{2,1,0:T(2,128)S(1)} %get-tuple-element.19), kind=kOutput, calls=%fused_computation.26 | convolution fusion | flops 811859968 | bytes 13901824 | tf_op jit(solution)/shard_map/hgqk,khd->qhgd/dot_general | solution.py:124
  186.2 7.5 %convolution_convert_fusion = bf16[512,5376]{1,0:T(8,128)(2,1)} fusion(bf16[512,512]{0,1:T(8,128)(2,1)S(1)} %bitcast.64, bf16[512,5376]{0,1:T(8,128)(2,1)} %all-gather.5.cloned.1.call-done), kind=kOutput, calls=%fused_computation.5 | convolution fusion | flops 2821324800 | bytes 11534336 | tf_op jit(solution)/shard_map/dot_general | solution.py:128
  193.7 42.8 %reduce-scatter.2.cloned.1.call-done = bf16[64,5376]{1,0:T(8,128)(2,1)} async-done(((bf16[512,5376]{1,0:T(8,128)(2,1)}), bf16[64,5376]{1,0:T(8,128)(2,1)}) %reduce-scatter.2.cloned.1.call-update) | async-done | bytes 688144 | tf_op jit(solution)/shard_map/reduce_scatter | solution.py:133
  237.9 2.3 fusion.14
  (47 shorter events, 10.8 us)
Async XLA Ops:
  6.5 88.2 %all-gather.3.cloned.1.call-start = ((), (), s32[]{:S(2)}) async-start(), calls=%async_computation.2 | async-start | bytes 11698176 | tf_op jit(solution)/shard_map/all_gather | solution.py:18
  14.2 85.6 %all-to-all-start = ((bf16[8,64,5376]{2,1,0:T(8,128)(2,1)}), bf16[8,64,5376]{2,1,0:T(8,128)(2,1)}, u32[]{:S(2)}, u32[]{:S(2)}) async-start(bf16[8,64,5376]{2,1,0:T(8,128)(2,1)} %stack.2), calls=%async_computation | async-start | bytes 11010048 | tf_op jit(solution)/shard_map/all_to_all | solution.py:62
  18.8 167.3 %all-gather.5.cloned.1.call-start = ((), (), s32[]{:S(2)}) async-start(), calls=%async_computation.3 | async-start | bytes 5849088 | tf_op jit(solution)/shard_map/all_gather | solution.py:130
  19.6 216.9 %reduce-scatter.2.cloned.1.call-start = ((), (), s32[]{:S(2)}) async-start(), calls=%async_computation.4 | async-start | bytes 6193152 | tf_op jit(solution)/shard_map/reduce_scatter | solution.py:133
  99.7 5.1 %copy-start.4 = (f32[128]{0:T(128)S(1)}, f32[128]{0:T(128)}, u32[]{:S(2)}) copy-start(f32[128]{0:T(128)} %param.20) | copy-start | bytes 1540
  105.2 32.8 %collective-permute-start.2 = (bf16[512,256]{1,0:T(8,128)(2,1)S(1)}, bf16[512,256]{1,0:T(8,128)(2,1)}, u32[]{:S(2)}, u32[]{:S(2)}) collective-permute-start(bf16[512,256]{1,0:T(8,128)(2,1)S(1)} %copy.27), channel_id=1, source_target_pairs={{0,8},{8,16},{16,24},{24,32},{32,40},{40,48},{48,56},{56,64},{64,7... | collective-permute-start | bytes 786440 | tf_op jit(solution)/shard_map/ppermute | solution.py:24
  114.3 16.8 %copy-start.2 = (bf16[512,256]{1,0:T(8,128)(2,1)}, bf16[512,256]{1,0:T(8,128)(2,1)S(1)}, u32[]{:S(2)}) copy-start(bf16[512,256]{1,0:T(8,128)(2,1)S(1)} %fusion.16) | copy-start | bytes 786436
  114.3 26.8 %collective-permute-start = (bf16[512,256]{1,0:T(8,128)(2,1)S(1)}, bf16[512,256]{1,0:T(8,128)(2,1)}, u32[]{:S(2)}, u32[]{:S(2)}) collective-permute-start(bf16[512,256]{1,0:T(8,128)(2,1)S(1)} %fusion.16), channel_id=1, source_target_pairs={{0,8},{8,16},{16,24},{24,32},{32,40},{40,48},{48,56},{56,64},{64,7... | collective-permute-start | bytes 786440 | tf_op jit(solution)/shard_map/ppermute | solution.py:24
  131.1 6.7 %copy-start.5 = (f32[128]{0:T(128)S(1)}, f32[128]{0:T(128)}, u32[]{:S(2)}) copy-start(f32[128]{0:T(128)} %param.19) | copy-start | bytes 1540
  138.0 15.0 %collective-permute-start.3 = (bf16[512,256]{1,0:T(8,128)(2,1)}, bf16[512,256]{1,0:T(8,128)(2,1)}, u32[]{:S(2)}, u32[]{:S(2)}) collective-permute-start(bf16[512,256]{1,0:T(8,128)(2,1)} %collective-permute-done.2), channel_id=1, source_target_pairs={{0,8},{8,16},{16,24},{24,32},{32,40},{40,48},{48,56},{56,64},{64,7... | collective-permute-start | bytes 786440 | tf_op jit(solution)/shard_map/ppermute | solution.py:24
  141.1 22.6 %collective-permute-start.1 = (bf16[512,256]{1,0:T(8,128)(2,1)}, bf16[512,256]{1,0:T(8,128)(2,1)}, u32[]{:S(2)}, u32[]{:S(2)}) collective-permute-start(bf16[512,256]{1,0:T(8,128)(2,1)} %collective-permute-done), channel_id=1, source_target_pairs={{0,8},{8,16},{16,24},{24,32},{32,40},{40,48},{48,56},{56,64},{64,7... | collective-permute-start | bytes 786440 | tf_op jit(solution)/shard_map/ppermute | solution.py:24
  169.9 10.7 %copy-start.1 = (bf16[1536,256]{0,1:T(8,128)(2,1)S(1)}, bf16[1536,256]{0,1:T(8,128)(2,1)}, u32[]{:S(2)}) copy-start(bf16[1536,256]{0,1:T(8,128)(2,1)} %copy.26) | copy-start | bytes 2359300
  193.7 44.1 %copy-start = (bf16[64,5376]{1,0:T(8,128)(2,1)S(1)}, bf16[64,5376]{1,0:T(8,128)(2,1)}, u32[]{:S(2)}) copy-start(bf16[64,5376]{1,0:T(8,128)(2,1)} %param.12) | copy-start | bytes 2064388
  193.7 44.2 %copy-start.3 = (f32[5376]{0:T(1024)S(1)}, f32[5376]{0:T(1024)}, u32[]{:S(2)}) copy-start(f32[5376]{0:T(1024)} %param.23) | copy-start | bytes 64516
Sparse Core Ops, SparseCore 0:
  9.5 85.2 all-gather.2
  96.9 74.3 all-gather.4
  193.9 42.6 reduce-scatter.1
